TPU v7x, 32 devices: a whole 2x2x4 slice. The times are simulated.
32 devices in a mesh: gx: 4 (over x, core), gy: 8 (over z, y).
Axes of the slice: x: 2, y: 2, z: 4, core: 2. Of those that a mesh axis runs over, the one named last changes fastest.
Arguments:
- state: float32 [512, 512, 128], P('gx', 'gy'), may hold values from -6 to 6
- diffusion: float32 [512, 512, 128], P('gx', 'gy'), may hold values from 0.01 to 0.12
- vert_inverse: float32 [512, 128, 128], P('gy'), as said below
- profiles: bfloat16 [8192, 128], P(('gx', 'gy')), may hold values from -6 to 6
- counts: int32 [32, 32], P(('gx', 'gy')), may hold values from 0 to 16, as said below
- cell_lon: int32 [8192], P(('gx', 'gy')), may hold values from 0 to 127
- cell_lat: int32 [8192], P(('gx', 'gy')), may hold values from 0 to 63
- weight_slot: int32 [2, 8192], P(None, ('gx', 'gy')), may hold values from 0 to 63
Outputs:
- adjoint: float32 [512, 512, 128], P('gx', 'gy')
Inputs may be any that keep to these rules, and one draw needn't show every extreme that they name: Each row s sums to 256; source device s stores its profiles in order of subdomain, counts[s,d] of them for subdomain d, which covers longitude cells (d // 8) * 128 onwards and latitude cells (d % 8) * 64 onwards. Some subdomain receives 16 profiles from every source. `vert_inverse`: one matrix for each latitude row.
All inputs are finite; a program needn't handle non-finite values.
Results may differ from a plain program's by a relative error of at most 0.0015.
Values may be sent and summed in bfloat16 or wider, within the bound.
A program may use at most 128 MiB of HBM per device.

v0:
```python
import functools

import jax
import jax.numpy as jnp
from jax import lax
from jax.experimental import pallas as pl
from jax.experimental.pallas import tpu as pltpu
from jax.sharding import PartitionSpec as P

CAP = 16
STEPS = 4
SLOTS = 64
EDGE = 8
F32 = jnp.float32
BF16 = jnp.bfloat16
MESH = pl.DeviceIdType.MESH
VMEM_LIMIT = 60 * 1024 * 1024


def pack_kernel(prof_ref, counts_ref, lon_ref, lat_ref, slot_ref, out_ref):
    rows_out = out_ref.shape[0]
    obs, levels = prof_ref.shape
    n_dest = counts_ref.shape[1]
    count_row = counts_ref[...].astype(F32)
    dest = lax.broadcasted_iota(jnp.int32, (rows_out, n_dest), 0) // CAP
    lane = lax.broadcasted_iota(jnp.int32, (rows_out, n_dest), 1)
    start = jnp.sum(jnp.where(lane < dest, count_row, 0.0), axis=1, keepdims=True)
    count = jnp.sum(jnp.where(lane == dest, count_row, 0.0), axis=1, keepdims=True)
    slot = (lax.broadcasted_iota(jnp.int32, (rows_out, 1), 0) % CAP).astype(F32)
    source = jnp.where(slot < count, start + slot, -1.0).astype(jnp.int32)
    column = lax.broadcasted_iota(jnp.int32, (rows_out, obs), 1)
    selector = jnp.where(column == source, 1.0, 0.0).astype(BF16)
    kind = lax.broadcasted_iota(jnp.int32, (levels, obs), 0)
    meta = jnp.where(kind == 0, lon_ref[...].astype(F32), 0.0)
    meta = jnp.where(kind == 1, lat_ref[...].astype(F32), meta)
    meta = jnp.where(kind == 2, slot_ref[0:1, :].astype(F32), meta)
    meta = jnp.where(kind == 3, slot_ref[1:2, :].astype(F32), meta)
    out_ref[:, 0:levels] = jnp.dot(
        selector, prof_ref[...], preferred_element_type=F32
    ).astype(BF16)
    out_ref[:, levels:] = lax.dot_general(
        selector, meta.astype(BF16), (((1,), (1,)), ((), ())), preferred_element_type=F32
    ).astype(BF16)


def split(value):
    upper = value.astype(BF16)
    return upper, (value - upper.astype(F32)).astype(BF16)


def step_kernel(
    n_gx, n_gy, group,
    msg_ref, state_hbm, diff_hbm, inv_hbm, out_hbm,
    st, df, wf, wst, mbuf, fbuf, obuf, wx_ref, table, scaled, col_send, col_recv,
    row_send, row_recv, xs, xr, yr,
    in_sem, out_sem, f_send, f_recv, x_send, x_recv, y_send, y_recv,
):
    lat, lon, levels = mbuf.shape
    slots = msg_ref.shape[0]
    gx, gy = lax.axis_index("gx"), lax.axis_index("gy")
    east = (lax.rem(gx + 1, n_gx), gy)
    west = (lax.rem(gx + n_gx - 1, n_gx), gy)
    north = (gx, lax.rem(gy + 1, n_gy))
    south = (gx, lax.rem(gy + n_gy - 1, n_gy))

    loads = [
        pltpu.make_async_copy(src, dst, in_sem.at[i])
        for i, (src, dst) in enumerate(((state_hbm, st), (inv_hbm, wf), (diff_hbm, df)))
    ]
    for load in loads:
        load.start()

    barrier = pltpu.get_barrier_semaphore()
    for peer in (east, west, north, south):
        pl.semaphore_signal(barrier, inc=1, device_id=peer, device_id_type=MESH)

    meta = jnp.transpose(msg_ref[:, levels:].astype(F32))
    lon_row, lat_row = meta[0:1, :], meta[1:2, :]
    frac_x = meta[2:3, :] / SLOTS
    frac_y = msg_ref[:, levels + 3 : levels + 4].astype(F32) / SLOTS
    values = msg_ref[:, 0:levels].astype(F32)
    for half, part in enumerate((values * (1.0 - frac_y), values * frac_y)):
        upper, lower = split(part)
        scaled[half * slots : (half + 1) * slots, 0:levels] = upper
        scaled[half * slots : (half + 1) * slots, levels:] = lower
    x_ids = lax.broadcasted_iota(jnp.int32, (lon, slots), 0).astype(F32)
    wx_ref[...] = jnp.where(x_ids == lon_row, 1.0 - frac_x, 0.0) + jnp.where(
        x_ids == lon_row + 1.0, frac_x, 0.0
    )

    def fold(product):
        return product[:, 0:levels] + product[:, levels:]

    col_rows = col_send.shape[0]
    y_ids = lax.broadcasted_iota(jnp.int32, (col_rows, slots), 0).astype(F32)
    last = jnp.where(lon_row == lon - 1.0, frac_x, 0.0)
    table[0:col_rows, 0:slots] = jnp.where(y_ids == lat_row, last, 0.0).astype(BF16)
    table[0:col_rows, slots:] = jnp.where(y_ids == lat_row + 1.0, last, 0.0).astype(BF16)
    col_send[...] = fold(
        jnp.dot(table[0:col_rows, :], scaled[...], preferred_element_type=F32)
    )
    pl.semaphore_wait(barrier, 4)
    col_copy = pltpu.make_async_remote_copy(
        src_ref=col_send, dst_ref=col_recv, send_sem=f_send.at[0], recv_sem=f_recv.at[0],
        device_id=east, device_id_type=MESH,
    )
    col_copy.start()

    first_x = lax.broadcasted_iota(jnp.int32, (lon, levels), 0) == 0
    table[0:lon, 0:slots] = jnp.zeros((lon, slots), BF16)
    table[0:lon, slots:] = jnp.where(lat_row == lat - 1.0, wx_ref[...], 0.0).astype(BF16)
    over = fold(jnp.dot(table[0:lon, :], scaled[...], preferred_element_type=F32))
    col_copy.wait()
    row_send[...] = over + jnp.where(first_x, col_recv[lat : lat + 1, :], 0.0)
    row_copy = pltpu.make_async_remote_copy(
        src_ref=row_send, dst_ref=row_recv, send_sem=f_send.at[1], recv_sem=f_recv.at[1],
        device_id=north, device_id_type=MESH,
    )
    row_copy.start()

    def force(index, carry):
        for j in range(group):
            here = (index * group + j).astype(F32)
            rows = slice(j * lon, (j + 1) * lon)
            table[rows, 0:slots] = jnp.where(lat_row == here, wx_ref[...], 0.0).astype(BF16)
            table[rows, slots:] = jnp.where(lat_row + 1.0 == here, wx_ref[...], 0.0).astype(BF16)
        total = fold(jnp.dot(table[...], scaled[...], preferred_element_type=F32))
        for j in range(group):
            y = index * group + j
            mbuf[y] = total[j * lon : (j + 1) * lon] + jnp.where(
                first_x, col_recv[pl.ds(y, 1), :], 0.0
            )
        return carry

    lax.fori_loop(0, lat // group, force, 0)
    row_copy.wait()
    mbuf[0] = mbuf[0] + jnp.where(gy > 0, row_recv[...], 0.0)

    middle = (lat // 2) // EDGE * EDGE
    chunks = ((0, EDGE), (lat - EDGE, lat), (EDGE, middle), (middle, lat - EDGE))
    last_x = lax.broadcasted_iota(jnp.int32, (lon, levels), 0) == lon - 1

    def x_copies(step, chunk):
        low, high = chunks[chunk]
        copies = []
        for side, peer in ((0, west), (1, east)):
            k = (step * 2 + side) * len(chunks) + chunk
            copies.append(
                pltpu.make_async_remote_copy(
                    src_ref=xs.at[step % 2, side, pl.ds(low, high - low)],
                    dst_ref=xr.at[step, 1 - side, pl.ds(low, high - low)],
                    send_sem=x_send.at[k], recv_sem=x_recv.at[k],
                    device_id=peer, device_id_type=MESH,
                )
            )
        return copies

    def y_copies(step):
        copies = []
        for side, peer in ((0, south), (1, north)):
            k = step * 2 + side
            copies.append(
                pltpu.make_async_remote_copy(
                    src_ref=fbuf.at[step % 2, lat if side else 1],
                    dst_ref=yr.at[step, 1 - side],
                    send_sem=y_send.at[k], recv_sem=y_recv.at[k],
                    device_id=peer, device_id_type=MESH,
                )
            )
        return copies

    def advanced(step, y):
        old = step % 2
        centre = fbuf[old, y + 1]
        behind = jnp.where(first_x, xr[step, 0, pl.ds(y, 1), :], pltpu.roll(centre, 1, 0))
        ahead = jnp.where(last_x, xr[step, 1, pl.ds(y, 1), :], pltpu.roll(centre, lon - 1, 0))
        return mbuf[y] + ((behind + ahead) + (fbuf[old, y] + fbuf[old, y + 2]))

    def section(step, y):
        if step == 0:
            lam = st[pl.ds(y, lon, stride=lat), :] + mbuf[y]
            pair = jnp.concatenate(split(wf[y]), axis=1)
            wst[y] = pair
        else:
            lam = advanced(step - 1, y)
            pair = wst[y]
        mixed = fold(
            jnp.dot(
                jnp.concatenate(split(lam), axis=1),
                jnp.concatenate([pair, pair], axis=0),
                preferred_element_type=F32,
            )
        )
        flux = df[pl.ds(y, lon, stride=lat), :] * mixed
        mbuf[y] = mixed - 4.0 * flux
        fbuf[step % 2, y + 1] = flux
        xs[step % 2, 0, pl.ds(y, 1), :] = flux[0:1]
        xs[step % 2, 1, pl.ds(y, 1), :] = flux[lon - 1 : lon]

    def sweep(work, low, high):
        def two(index, carry):
            work(low + 2 * index)
            work(low + 2 * index + 1)
            return carry

        lax.fori_loop(0, (high - low) // 2, two, 0)

    def halo(step):
        for copy in y_copies(step):
            copy.wait()
        fbuf[step % 2, 0] = jnp.where(gy > 0, yr[step, 0], 0.0)
        fbuf[step % 2, lat + 1] = jnp.where(gy < n_gy - 1, yr[step, 1], 0.0)

    for load in loads:
        load.wait()
    for step in range(STEPS):
        if step:
            halo(step - 1)
        for chunk, (low, high) in enumerate(chunks):
            if step:
                for copy in x_copies(step - 1, chunk):
                    copy.wait()
            sweep(functools.partial(section, step), low, high)
            if chunk == 1:
                for copy in y_copies(step):
                    copy.start()
            for copy in x_copies(step, chunk):
                copy.start()

    def finish(y):
        obuf[y] = advanced(STEPS - 1, y)

    halo(STEPS - 1)
    stores = []
    for chunk, (low, high) in enumerate(chunks):
        for copy in x_copies(STEPS - 1, chunk):
            copy.wait()
        sweep(finish, low, high)
        part = pl.ds(low, high - low)
        stores.append(pltpu.make_async_copy(obuf.at[part], out_hbm.at[part], out_sem.at[chunk]))
        stores[-1].start()
    for store in stores:
        store.wait()


def solution(mesh):
    n_gx, n_gy = mesh.shape["gx"], mesh.shape["gy"]

    def shards(state, diffusion, vert_inverse, profiles, counts, cell_lon, cell_lat, weight_slot):
        lon, lat, levels = state.shape
        n_dest = counts.shape[1]
        slots = n_dest * CAP
        group = 4
        message = pl.pallas_call(
            pack_kernel,
            out_shape=jax.ShapeDtypeStruct((slots, 2 * levels), BF16),
            compiler_params=pltpu.CompilerParams(vmem_limit_bytes=VMEM_LIMIT),
            name="pack",
        )(profiles, counts, cell_lon[None], cell_lat[None], weight_slot)
        message = lax.all_to_all(
            message.reshape(n_dest, CAP, 2 * levels), ("gx", "gy"),
            split_axis=0, concat_axis=0, tiled=True,
        ).reshape(slots, 2 * levels)
        n_x = STEPS * 2 * 4
        dma = pltpu.SemaphoreType.DMA
        out = pl.pallas_call(
            functools.partial(step_kernel, n_gx, n_gy, group),
            out_shape=jax.ShapeDtypeStruct((lat, lon, levels), F32),
            in_specs=[pl.BlockSpec(memory_space=pltpu.VMEM)]
            + [pl.BlockSpec(memory_space=pl.ANY)] * 3,
            out_specs=pl.BlockSpec(memory_space=pl.ANY),
            scratch_shapes=[
                pltpu.VMEM((lon * lat, levels), F32),
                pltpu.VMEM((lon * lat, levels), F32),
                pltpu.VMEM((lat, levels, levels), F32),
                pltpu.VMEM((lat, levels, 2 * levels), BF16),
                pltpu.VMEM((lat, lon, levels), F32),
                pltpu.VMEM((2, lat + 2, lon, levels), F32),
                pltpu.VMEM((lat, lon, levels), F32),
                pltpu.VMEM((lon, slots), F32),
                pltpu.VMEM((group * lon, 2 * slots), BF16),
                pltpu.VMEM((2 * slots, 2 * levels), BF16),
                pltpu.VMEM((lat + 8, levels), F32),
                pltpu.VMEM((lat + 8, levels), F32),
                pltpu.VMEM((lon, levels), F32),
                pltpu.VMEM((lon, levels), F32),
                pltpu.VMEM((2, 2, lat, levels), F32),
                pltpu.VMEM((STEPS, 2, lat, levels), F32),
                pltpu.VMEM((STEPS, 2, lon, levels), F32),
                dma((3,)), dma((4,)), dma((2,)), dma((2,)),
                dma((n_x,)), dma((n_x,)), dma((STEPS * 2,)), dma((STEPS * 2,)),
            ],
            compiler_params=pltpu.CompilerParams(
                collective_id=0, has_side_effects=True, vmem_limit_bytes=VMEM_LIMIT
            ),
            name="steps",
        )(
            message,
            state.reshape(lon * lat, levels),
            diffusion.reshape(lon * lat, levels),
            vert_inverse,
        )
        return jnp.transpose(out, (1, 0, 2))

    return jax.shard_map(
        shards,
        mesh=mesh,
        in_specs=(
            P("gx", "gy", None),
            P("gx", "gy", None),
            P("gy", None, None),
            P(("gx", "gy"), None),
            P(("gx", "gy"), None),
            P(("gx", "gy")),
            P(("gx", "gy")),
            P(None, ("gx", "gy")),
        ),
        out_specs=P("gx", "gy", None),
        check_vma=False,
    )
```

profile of v0, /device:TPU:1, one launch (start us, length us, event | category | flops | bytes accessed | tf_op | source)
XLA Modules:
  0.0 69.8 jit_solution(5741191121798369952)
XLA Ops:
  0.0 1.9 %pack.1 = bf16[512,256]{1,0:T(8,128)(2,1)} custom-call(bf16[256,128]{1,0:T(8,128)(2,1)} %prof_ref.1, s32[1,32]{1,0:T(1,128)} %counts_ref.1, s32[1,256]{1,0:T(1,128)} %bitcast.12, s32[1,256]{1,0:T(1,128)} %bitcast.13, s32[2,256]{1,0:T(2,128)} %slot_ref.1), custom_call_target="tpu_custom_call" | custom-call | tf_op jit(solution)/shard_map/pack/pallas_call | solution.py:254
  1.9 17.3 %all_to_all.5 = bf16[32,16,256]{2,1,0:T(8,128)(2,1)} all-to-all(bf16[32,16,256]{2,1,0:T(8,128)(2,1)} %bitcast.11), channel_id=1, replica_groups=mesh['gx'=4,'gy'=8] {'gx','gy'}, dimensions={0} | all-to-all | bytes 524288 | tf_op jit(solution)/shard_map/all_to_all | solution.py:260
  19.3 43.9 %steps.1 = f32[64,128,128]{2,1,0:T(8,128)} custom-call(bf16[512,256]{1,0:T(8,128)(2,1)} %bitcast.10, f32[8192,128]{1,0:T(8,128)} %bitcast.8, f32[8192,128]{1,0:T(8,128)} %bitcast.9, f32[64,128,128]{2,1,0:T(8,128)} %inv_hbm.1), custom_call_target="tpu_custom_call" | custom-call | tf_op jit(solution)/shard_map/steps/pallas_call | solution.py:266
  63.2 6.6 %copy.9 = f32[128,64,128]{2,1,0:T(8,128)} copy(f32[128,64,128]{2,0,1:T(8,128)} %bitcast.7) | data formatting | bytes 8388608 | tf_op jit(solution)/shard_map/transpose | solution.py:303
where the time goes:
time: 70.1 us; the launch traced here: 69.8 us
  Pallas kernels  45.8 us (65%)
  blocking collectives  17.3 us (25%)
  local copies, waits for them, and re-layouts  6.63 us (9%)
    pallas_call x1, Pallas kernels, shards(): pl.pallas_call(functools.partial(step_kernel, n_gx, n_gy, group), out_sha...  43.9 us
    all_to_all x1, blocking collectives, shards(): lax.all_to_all(message.reshape(n_dest, CAP, 2 * levels), ('gx', 'gy'), sp...  17.3 us
    transpose x1, local copies, waits for them, and re-layouts, shards(): return jnp.transpose(out, (1, 0, 2))  6.63 us
    pallas_call x1, Pallas kernels, shards(): pl.pallas_call(pack_kernel, out_shape=jax.ShapeDtypeStruct((slots, 2 * le...  1.94 us

commit v1 on v0

--- a/solution.py
+++ b/solution.py
@@ -17,8 +17,24 @@
 VMEM_LIMIT = 60 * 1024 * 1024
 
 
-def pack_kernel(prof_ref, counts_ref, lon_ref, lat_ref, slot_ref, out_ref):
-    rows_out = out_ref.shape[0]
+def pack_kernel(
+    n_gy, prof_ref, counts_ref, lon_ref, lat_ref, slot_ref, out_ref, msg, recv, send_sem, recv_sem
+):
+    n_all = msg.shape[0]
+    me = lax.axis_index("gx") * n_gy + lax.axis_index("gy")
+
+    def peer(offset):
+        other = lax.rem(me + offset, n_all)
+        return other, (other // n_gy, lax.rem(other, n_gy))
+
+    barrier = pltpu.get_barrier_semaphore()
+
+    def greet(offset, carry):
+        pl.semaphore_signal(barrier, inc=1, device_id=peer(offset)[1], device_id_type=MESH)
+        return carry
+
+    lax.fori_loop(1, n_all, greet, 0)
+    rows_out = n_all * CAP
     obs, levels = prof_ref.shape
     n_dest = counts_ref.shape[1]
     count_row = counts_ref[...].astype(F32)
@@ -35,12 +51,40 @@
     meta = jnp.where(kind == 1, lat_ref[...].astype(F32), meta)
     meta = jnp.where(kind == 2, slot_ref[0:1, :].astype(F32), meta)
     meta = jnp.where(kind == 3, slot_ref[1:2, :].astype(F32), meta)
-    out_ref[:, 0:levels] = jnp.dot(
-        selector, prof_ref[...], preferred_element_type=F32
-    ).astype(BF16)
-    out_ref[:, levels:] = lax.dot_general(
-        selector, meta.astype(BF16), (((1,), (1,)), ((), ())), preferred_element_type=F32
-    ).astype(BF16)
+    msg[:, :, 0:levels] = (
+        jnp.dot(selector, prof_ref[...], preferred_element_type=F32)
+        .astype(BF16)
+        .reshape(n_all, CAP, levels)
+    )
+    msg[:, :, levels:] = (
+        lax.dot_general(
+            selector, meta.astype(BF16), (((1,), (1,)), ((), ())), preferred_element_type=F32
+        )
+        .astype(BF16)
+        .reshape(n_all, CAP, levels)
+    )
+    pl.semaphore_wait(barrier, n_all - 1)
+
+    def block_copy(offset):
+        other, device = peer(offset)
+        return pltpu.make_async_remote_copy(
+            src_ref=msg.at[other], dst_ref=recv.at[me],
+            send_sem=send_sem.at[offset], recv_sem=recv_sem.at[offset],
+            device_id=device, device_id_type=MESH,
+        )
+
+    def send(offset, carry):
+        block_copy(offset).start()
+        return carry
+
+    def arrive(offset, carry):
+        block_copy(offset).wait()
+        return carry
+
+    lax.fori_loop(1, n_all, send, 0)
+    recv[me] = msg[me]
+    lax.fori_loop(1, n_all, arrive, 0)
+    out_ref[...] = recv[...]
 
 
 def split(value):
@@ -251,16 +295,22 @@
         n_dest = counts.shape[1]
         slots = n_dest * CAP
         group = 4
+        block = (n_dest, CAP, 2 * levels)
         message = pl.pallas_call(
-            pack_kernel,
-            out_shape=jax.ShapeDtypeStruct((slots, 2 * levels), BF16),
-            compiler_params=pltpu.CompilerParams(vmem_limit_bytes=VMEM_LIMIT),
+            functools.partial(pack_kernel, n_gy),
+            out_shape=jax.ShapeDtypeStruct(block, BF16),
+            scratch_shapes=[
+                pltpu.VMEM(block, BF16),
+                pltpu.VMEM(block, BF16),
+                pltpu.SemaphoreType.DMA((n_dest,)),
+                pltpu.SemaphoreType.DMA((n_dest,)),
+            ],
+            compiler_params=pltpu.CompilerParams(
+                collective_id=1, has_side_effects=True, vmem_limit_bytes=VMEM_LIMIT
+            ),
             name="pack",
         )(profiles, counts, cell_lon[None], cell_lat[None], weight_slot)
-        message = lax.all_to_all(
-            message.reshape(n_dest, CAP, 2 * levels), ("gx", "gy"),
-            split_axis=0, concat_axis=0, tiled=True,
-        ).reshape(slots, 2 * levels)
+        message = message.reshape(slots, 2 * levels)
         n_x = STEPS * 2 * 4
         dma = pltpu.SemaphoreType.DMA
         out = pl.pallas_call(

time: 70.1 us -> 67.5 us (0.963)
  blocking collectives: 17.3 us -> 0 us
  Pallas kernels: 45.8 us -> 60.6 us
    all_to_all x1 -> x0, blocking collectives: 17.3 us -> none  [shards(): lax.all_to_all(message.reshape(n_dest, CAP, 2 * levels), ('gx', 'gy'), sp...]
    pallas_call x1, Pallas kernels: 1.94 us -> 15.4 us  [shards(): pl.pallas_call(functools.partial(pack_kernel, n_gy), out_shape=jax.ShapeD...]
    pallas_call x1, Pallas kernels: 43.9 us -> 45.3 us  [shards(): pl.pallas_call(functools.partial(step_kernel, n_gx, n_gy, group), out_sha...]
where the time goes in v1:
time: 67.5 us; the launch traced here: 67.3 us
  Pallas kernels  60.6 us (90%)
  local copies, waits for them, and re-layouts  6.63 us (10%)
    pallas_call x1, Pallas kernels, shards(): pl.pallas_call(functools.partial(step_kernel, n_gx, n_gy, group), out_sha...  45.3 us
    pallas_call x1, Pallas kernels, shards(): pl.pallas_call(functools.partial(pack_kernel, n_gy), out_shape=jax.ShapeD...  15.4 us
    transpose x1, local copies, waits for them, and re-layouts, shards(): return jnp.transpose(out, (1, 0, 2))  6.63 us

profile of v1, /device:TPU:1, one launch (start us, length us, event | category | flops | bytes accessed | tf_op | source)
XLA Modules:
  0.0 67.3 jit_solution(12842160380472667290)
XLA Ops:
  0.0 15.4 %pack.1 = bf16[32,16,256]{2,1,0:T(8,128)(2,1)} custom-call(bf16[256,128]{1,0:T(8,128)(2,1)} %prof_ref.1, s32[1,32]{1,0:T(1,128)} %counts_ref.1, s32[1,256]{1,0:T(1,128)} %bitcast.10, s32[1,256]{1,0:T(1,128)} %bitcast.11, s32[2,256]{1,0:T(2,128)} %slot_ref.1), custom_call_target="tpu_custom_call" | custom-call | tf_op jit(solution)/shard_map/pack/pallas_call | solution.py:299
  15.4 45.3 %steps.1 = f32[64,128,128]{2,1,0:T(8,128)} custom-call(bf16[512,256]{1,0:T(8,128)(2,1)} %bitcast.9, f32[8192,128]{1,0:T(8,128)} %bitcast.7, f32[8192,128]{1,0:T(8,128)} %bitcast.8, f32[64,128,128]{2,1,0:T(8,128)} %inv_hbm.1), custom_call_target="tpu_custom_call" | custom-call | tf_op jit(solution)/shard_map/steps/pallas_call | solution.py:316
  60.7 6.6 %copy.9 = f32[128,64,128]{2,1,0:T(8,128)} copy(f32[128,64,128]{2,0,1:T(8,128)} %bitcast.6) | data formatting | bytes 8388608 | tf_op jit(solution)/shard_map/transpose | solution.py:353
